TPU v7x, 256 devices: a whole 4x4x8 slice. The times are simulated.
256 devices in a mesh: rep: 32 (over x, z_lo, y), shard: 8 (over z_hi, core).
Axes of the slice: x: 4, y: 4, z: 8 (z_hi: 4, z_lo: 2; z = z_hi * 2 + z_lo), core: 2. Of those that a mesh axis runs over, the one named last changes fastest.
Arguments:
- params: float32 [32, 1600, 3200], P('rep', None, 'shard'), may hold values from -6 to 6
- momentum: float32 [32, 1600, 3200], P('rep', None, 'shard'), may hold values from -6 to 6
- tokens: bfloat16 [32, 2, 1024, 1600], P('rep', None, 'shard'), may hold values from -6 to 6
- targets: bfloat16 [32, 2, 1024, 3200], P('rep', None, None, 'shard'), may hold values from -6 to 6
- blend_weight: float32 [3200], P('shard'), may hold values from 0.2 to 0.9
Outputs:
- averaged: float32 [1600, 3200], P(None, 'shard')
- blended: float32 [32, 1600, 3200], P('rep', None, 'shard')
All inputs are finite; a program needn't handle non-finite values.
Results may differ from a plain program's by a relative error of at most 0.0045.
Values may be sent and summed in bfloat16 or wider, within the bound.
A program may use at most 128 MiB of HBM per device.

v0:
```python
import jax
import jax.numpy as jnp
from jax import lax
from jax.sharding import PartitionSpec as P

D = 1600
learn_rate = 0.05
momentum_decay = 0.9


def in_blocks(shard, dim, count):
    before, after = (shard.shape[:dim], shard.shape[dim + 1 :])
    return jnp.moveaxis(shard.reshape(*before, count, -1, *after), dim, 0)


def sum_together(arrays, axis, dims):
    count = lax.axis_size(axis)
    parts = [in_blocks(a, dim, count) for a, dim in zip(arrays, dims)]
    lines = jnp.concatenate([b.reshape(count, -1) for b in parts], axis=1)
    rows = max(16, -(-lines.shape[1] // 1024) * 8)
    lines = jnp.pad(lines, ((0, 0), (0, rows * 128 - lines.shape[1]))).reshape(-1, 128)
    flat, at, gathered = (lax.psum_scatter(lines, axis, tiled=True).reshape(-1), 0, [])
    for b in parts:
        part = b[0]
        gathered.append(flat[at : at + part.size].reshape(part.shape))
        at += part.size
    return tuple(gathered)


def in_one_piece(arrays, axis, dim, along):
    ends, at = ([], 0)
    for a in arrays[:-1]:
        at += a.shape[along]
        ends.append(at)
    both = jnp.concatenate(arrays, axis=along)
    return tuple(jnp.split(lax.all_gather(both, axis, axis=dim, tiled=True), ends, axis=along))


def gelu_tanh(value):
    return jax.nn.gelu(value, approximate=True)


def local(params, momentum, tokens, targets, blend_weight):
    inputs = lax.all_gather(tokens[0], "shard", axis=1, tiled=True)
    wanted = targets[0]
    weight = params[0]
    moment = momentum[0]
    scaling = 1.0 / jnp.sqrt(jnp.float32(D))
    for local_step in range(inputs.shape[0]):
        weight_half = weight.astype(jnp.bfloat16)
        pre = jnp.dot(inputs[local_step], weight_half, preferred_element_type=jnp.float32) * scaling
        activation, pullback = jax.vjp(gelu_tanh, pre)
        (slope,) = pullback(activation - wanted[local_step].astype(jnp.float32))
        hidden_grad = (slope * scaling).astype(jnp.bfloat16)
        gradient = lax.dot_general(
            inputs[local_step],
            hidden_grad,
            (((0,), (0,)), ((), ())),
            preferred_element_type=jnp.float32,
        )
        moment = momentum_decay * moment + gradient
        weight = weight - learn_rate * moment
    replicas = lax.axis_size("rep")
    sum_weight, sum_moment = sum_together((weight, moment), "rep", (0, 0))
    averaged, mean_moment = in_one_piece(
        (sum_weight / jnp.float32(replicas), sum_moment / jnp.float32(replicas)), "rep", 0, 1
    )
    blended = blend_weight * mean_moment + (1.0 - blend_weight) * moment
    return (averaged, blended[None])


def solution(mesh):
    return jax.shard_map(
        local,
        mesh=mesh,
        in_specs=(
            P("rep", None, "shard"),
            P("rep", None, "shard"),
            P("rep", None, "shard", None),
            P("rep", None, None, "shard"),
            P("shard"),
        ),
        out_specs=(P(None, "shard"), P("rep", None, "shard")),
        check_vma=False,
    )
```

profile of v0, /device:TPU:8, one launch (start us, length us, event | category | flops | bytes accessed | tf_op | source)
XLA Modules:
  0.0 498.4 jit_solution(11711380897204350947)
XLA Ops:
  7.2 0.0 all-gather.5.cloned.1.call-start
  7.2 0.7 all-gather.5.cloned.1.call-update
  7.9 0.0 reduce-scatter.2.cloned.1.call-start
  8.0 81.2 %all-gather.5.cloned.1.call-done = bf16[1,2,1024,1600]{2,3,1,0:T(8,128)(2,1)} async-done(((bf16[1,2,128,1600]{2,3,1,0:T(8,128)(2,1)}), bf16[1,2,1024,1600]{2,3,1,0:T(8,128)(2,1)}) %all-gather.5.cloned.1.call-update) | async-done | bytes 6553616 | tf_op jit(solution)/shard_map/all_gather | solution.py:44
  89.2 10.5 %fusion = f32[1600,400]{0,1:T(8,128)} fusion(bf16[1,2,1024,1600]{2,3,1,0:T(8,128)(2,1)} %all-gather.5.cloned.1.call-done, f32[1,1600,400]{1,2,0:T(8,128)} %param.6, f32[1,1600,400]{1,2,0:T(8,128)} %param.5, bf16[1,2,1024,400]{2,3,1,0:T(8,128)(2,1)} %param.8), kind=kOutput, calls=%fused_computation.6 | convolution fusion | flops 2633600000 | bytes 15257600 | tf_op jit(solution)/shard_map/dot_general | solution.py:55
  99.6 11.8 %multiply_subtract_fusion = (f32[1600,400]{0,1:T(8,128)}, f32[1600,400]{0,1:T(8,128)}) fusion(f32[1600,400]{0,1:T(8,128)} %fusion, f32[1,1600,400]{1,2,0:T(8,128)S(1)} %copy-done.1, bf16[1,2,1024,1600]{2,3,1,0:T(8,128)(2,1)} %all-gather.5.cloned.1.call-done, bf16[1,2,1024,400]{2,3,1,0:T(8,128)(2,1)} %param.8), kind=kOutput, calls=%fused_computation.12 | convolution fusion | flops 2637440000 | bytes 23142400 | tf_op jit(solution)/shard_map/dot_general | solution.py:55
  111.4 3.3 copy.12
  114.7 2.0 reshape_reshape.7
  116.7 3.3 copy.11
  120.0 2.0 reshape_reshape.6
  122.1 5.7 %select_maximum_fusion = f32[32,40960]{1,0:T(8,128)} fusion(f32[32,20000]{1,0:T(8,128)} %reshape_reshape.7, f32[32,20000]{1,0:T(8,128)} %reshape_reshape.6), kind=kLoop, calls=%fused_computation | loop fusion | flops 5242880 | bytes 10362880 | tf_op jit(solution)/shard_map/concatenate | solution.py:19
  127.7 5.5 %reshape.29 = f32[10240,128]{1,0:T(8,128)} reshape(f32[32,40960]{1,0:T(8,128)} %select_maximum_fusion) | data formatting | bytes 10485760 | tf_op jit(solution)/shard_map/reshape | solution.py:21
  133.3 0.2 all-gather.7.cloned.1.call-start
  133.5 168.5 %reduce-scatter.2.cloned.1.call-done = f32[320,128]{1,0:T(8,128)} async-done(((f32[10240,128]{1,0:T(8,128)}), f32[320,128]{1,0:T(8,128)}) %reduce-scatter.2.cloned.1.call-update) | async-done | bytes 163856 | tf_op jit(solution)/shard_map/reduce_scatter | solution.py:22
  302.1 1.1 slice_multiply_fusion.1
  303.1 0.1 div.11
  303.3 0.1 div.13
  303.4 0.8 maximum_bitcast_fusion
  304.2 164.6 %all-gather.7.cloned.1.call-done = f32[32,50,800]{2,1,0:T(8,128)} async-done(((f32[1,50,800]{2,1,0:T(8,128)}), f32[32,50,800]{2,1,0:T(8,128)}) %all-gather.7.cloned.1.call-update) | async-done | bytes 5120016 | tf_op jit(solution)/shard_map/all_gather | solution.py:36
  468.8 5.8 %reshape.39 = f32[1600,800]{1,0:T(8,128)} reshape(f32[32,50,800]{2,1,0:T(8,128)} %all-gather.7.cloned.1.call-done) | data formatting | bytes 10240000
  474.7 5.6 %fusion.65 = (f32[1600,400]{1,0:T(8,128)}, f32[1600,400]{1,0:T(8,128)S(1)}) fusion(f32[1600,800]{1,0:T(8,128)} %reshape.39), kind=kLoop, calls=%fused_computation.82 | loop fusion | bytes 10240000 | tf_op jit(solution)/shard_map/split | solution.py:36
  480.3 4.4 copy.15
  484.7 2.7 copy.14
  487.5 4.4 add_bitcast_fusion
  (7 shorter events, 0.0 us)
Async XLA Ops:
  7.2 82.0 %all-gather.5.cloned.1.call-start = ((), (), s32[]{:S(2)}) async-start(), calls=%async_computation.2 | async-start | bytes 7372800 | tf_op jit(solution)/shard_map/all_gather | solution.py:44
  7.9 91.7 %copy-start.1 = (f32[1,1600,400]{1,2,0:T(8,128)S(1)}, f32[1,1600,400]{1,2,0:T(8,128)}, u32[]{:S(2)}) copy-start(f32[1,1600,400]{1,2,0:T(8,128)} %param.5) | copy-start | bytes 7680004
  7.9 294.2 %reduce-scatter.2.cloned.1.call-start = ((), (), s32[]{:S(2)}) async-start(), calls=%async_computation.1 | async-start | bytes 5406720 | tf_op jit(solution)/shard_map/reduce_scatter | solution.py:22
  133.3 170.9 %copy-start = (f32[400]{0:T(512)S(1)}, f32[400]{0:T(512)}, u32[]{:S(2)}) copy-start(f32[400]{0:T(512)} %param.9) | copy-start | bytes 4804
  133.3 335.5 %all-gather.7.cloned.1.call-start = ((), (), s32[]{:S(2)}) async-start(), calls=%async_computation.3 | async-start | bytes 6623232 | tf_op jit(solution)/shard_map/all_gather | solution.py:36
Sparse Core Ops, SparseCore 0:
  9.8 79.3 all-gather.4
  133.4 168.6 reduce-scatter.1
  304.4 164.3 all-gather.6
where the time goes:
time: 499 us; the launch traced here: 498 us
  waiting for transfers between devices  415 us (83%)
  local copies, waits for them, and re-layouts  35.1 us (7%)
  matrix products  22.2 us (4%)
  between operations  13.8 us (3%)
  other arithmetic  11.9 us (2%)
    reduce_scatter x1, waiting for transfers between devices, sum_together(): lax.psum_scatter(lines, axis, tiled=True).reshape(-1)  169 us
    all_gather x1, waiting for transfers between devices, in_one_piece(): lax.all_gather(both, axis, axis=dim, tiled=True)  165 us
    all_gather x1, waiting for transfers between devices, local(): inputs = lax.all_gather(tokens[0], 'shard', axis=1, tiled=True)  81.2 us
    dot_general x2, matrix products, local(): lax.dot_general(inputs[local_step], hidden_grad, (((0,), (0,)), ((), ()))...  22.2 us
    unnamed x7, local copies, waits for them, and re-layouts  13 us
  transfers between devices with their start and end apart: 3, of which 3 were waited for; matrix products, arithmetic and copies ran while one was open for 0% of the time, Pallas kernels for 0%

commit v1 on v0

--- a/solution.py
+++ b/solution.py
@@ -41,7 +41,9 @@
 
 
 def local(params, momentum, tokens, targets, blend_weight):
-    inputs = lax.all_gather(tokens[0], "shard", axis=1, tiled=True)
+    inputs = jnp.concatenate(
+        lax.all_to_all(jnp.stack([tokens[0]] * lax.axis_size("shard")), "shard", 0, 0), axis=1
+    )
     wanted = targets[0]
     weight = params[0]
     moment = momentum[0]

time: 499 us -> 594 us (1.19)
  blocking collectives: 0 us -> 156 us
  waiting for transfers between devices: 415 us -> 331 us
  local copies, waits for them, and re-layouts: 35.1 us -> 57.9 us
    all_to_all x0 -> x1, blocking collectives: none -> 156 us  [local(): lax.all_to_all(jnp.stack([tokens[0]] * lax.axis_size('shard')), 'shard',...]
    all_gather x1 -> x0, waiting for transfers between devices: 81.2 us -> none  [local(): inputs = lax.all_gather(tokens[0], 'shard', axis=1, tiled=True)]
    slice x0 -> x3, local copies, waits for them, and re-layouts: none -> 20.4 us  [local(): inputs[local_step]]
    unnamed x7 -> x5, local copies, waits for them, and re-layouts: 13 us -> 13 us
  transfers between devices with their start and end apart: 3 -> 2, of which waited for: 3 -> 2; matrix products, arithmetic and copies ran while one was open for 0% -> 0% of each run, Pallas kernels for 0% -> 0%
where the time goes in v1:
time: 594 us; the launch traced here: 593 us
  waiting for transfers between devices  331 us (56%)
  blocking collectives  156 us (26%)
  local copies, waits for them, and re-layouts  57.9 us (10%)
  matrix products  21.9 us (4%)
  between operations  14.1 us (2%)
  other arithmetic  11.9 us (2%)
    reduce_scatter x1, waiting for transfers between devices, sum_together(): lax.psum_scatter(lines, axis, tiled=True).reshape(-1)  167 us
    all_gather x1, waiting for transfers between devices, in_one_piece(): lax.all_gather(both, axis, axis=dim, tiled=True)  164 us
    all_to_all x1, blocking collectives, local(): lax.all_to_all(jnp.stack([tokens[0]] * lax.axis_size('shard')), 'shard',...  156 us
    dot_general x2, matrix products, local(): lax.dot_general(inputs[local_step], hidden_grad, (((0,), (0,)), ((), ()))...  21.9 us
    slice x3, local copies, waits for them, and re-layouts, local(): inputs[local_step]  20.4 us
    unnamed x5, local copies, waits for them, and re-layouts  13 us
  transfers between devices with their start and end apart: 2, of which 2 were waited for; matrix products, arithmetic and copies ran while one was open for 0% of the time, Pallas kernels for 0%

profile of v1, /device:TPU:8, one launch (start us, length us, event | category | flops | bytes accessed | tf_op | source)
XLA Modules:
  0.0 593.1 jit_solution(17262849090606644341)
XLA Ops:
  7.2 2.4 stack.3
  9.6 156.1 %all_to_all.5 = bf16[8,2,128,1600]{2,3,1,0:T(8,128)(2,1)S(1)} all-to-all(bf16[8,2,128,1600]{2,3,1,0:T(8,128)(2,1)S(1)} %stack.3), channel_id=1, replica_groups=mesh['rep'=32,'shard'=8] {'shard'}, dimensions={0} | all-to-all | bytes 13107200 | tf_op jit(solution)/shard_map/all_to_all | solution.py:45
  165.8 0.4 fusion.93
  166.2 10.5 %copy.17 = bf16[1,8,128,1600]{2,1,3,0:T(8,128)(2,1)} copy(bf16[1,8,128,1600]{2,3,0,1:T(8,128)(2,1)S(1)} %get-tuple-element.8) | data formatting | bytes 6553600 | tf_op jit(solution)/shard_map/slice | solution.py:58
  176.7 9.5 %copy.18 = bf16[1,8,128,1600]{2,1,3,0:T(8,128)(2,1)S(1)} copy(bf16[1,8,128,1600]{2,3,0,1:T(8,128)(2,1)S(1)} %get-tuple-element.9) | data formatting | bytes 6553600 | tf_op jit(solution)/shard_map/slice | solution.py:58
  186.2 10.5 %fusion.17 = f32[1600,400]{0,1:T(8,128)} fusion(bf16[200,8,8,128]{3,2,1,0:T(8,128)(2,1)} %bitcast.112, f32[1,1600,400]{1,2,0:T(8,128)} %param.6, f32[1,1600,400]{1,2,0:T(8,128)} %param.5, bf16[1,2,1024,400]{2,3,1,0:T(8,128)(2,1)} %param.8), kind=kOutput, calls=%fused_computation.13 | convolution fusion | flops 2633600000 | bytes 15257600 | tf_op jit(solution)/shard_map/dot_general | solution.py:57
  196.6 11.4 %multiply_subtract_fusion = (f32[1600,400]{0,1:T(8,128)}, f32[1600,400]{0,1:T(8,128)}) fusion(f32[1600,400]{0,1:T(8,128)} %fusion.17, f32[1,1600,400]{1,2,0:T(8,128)} %param.5, bf16[200,8,8,128]{3,2,1,0:T(8,128)(2,1)S(1)} %bitcast.111, bf16[1,2,1024,400]{2,3,1,0:T(8,128)(2,1)} %param.8), kind=kOutput, calls=%fused_computation.20 | convolution fusion | flops 2637440000 | bytes 23142400 | tf_op jit(solution)/shard_map/dot_general | solution.py:57
  208.0 3.3 copy.20
  211.3 2.0 reshape_reshape.7
  213.4 3.3 copy.19
  216.7 2.0 reshape_reshape.6
  218.7 5.7 select_maximum_fusion
  224.4 5.5 reshape.39
  230.0 166.7 %reduce-scatter.2.cloned.1.call-done = f32[320,128]{1,0:T(8,128)} async-done(((f32[10240,128]{1,0:T(8,128)}), f32[320,128]{1,0:T(8,128)}) %reduce-scatter.2.cloned.1.call-update) | async-done | bytes 163856 | tf_op jit(solution)/shard_map/reduce_scatter | solution.py:22
  396.7 1.1 slice_multiply_fusion.1
  397.7 0.1 div.11
  397.9 0.1 div.13
  398.0 0.8 maximum_bitcast_fusion
  398.8 164.3 %all-gather.3.cloned.1.call-done = f32[32,50,800]{2,1,0:T(8,128)} async-done(((f32[1,50,800]{2,1,0:T(8,128)}), f32[32,50,800]{2,1,0:T(8,128)}) %all-gather.3.cloned.1.call-update) | async-done | bytes 5120016 | tf_op jit(solution)/shard_map/all_gather | solution.py:36
  563.1 5.8 reshape.44
  569.0 5.6 fusion.94
  574.6 4.4 copy.23
  579.1 2.7 copy.22
  581.8 4.4 add_bitcast_fusion
  (7 shorter events, 0.1 us)
Async XLA Ops:
  7.2 389.5 %reduce-scatter.2.cloned.1.call-start = ((), (), s32[]{:S(2)}) async-start(), calls=%async_computation.2 | async-start | bytes 5406720 | tf_op jit(solution)/shard_map/reduce_scatter | solution.py:22
  229.9 168.9 %copy-start = (f32[400]{0:T(512)S(1)}, f32[400]{0:T(512)}, u32[]{:S(2)}) copy-start(f32[400]{0:T(512)} %param.9) | copy-start | bytes 4804
  229.9 333.2 %all-gather.3.cloned.1.call-start = ((), (), s32[]{:S(2)}) async-start(), calls=%async_computation.3 | async-start | bytes 6623232 | tf_op jit(solution)/shard_map/all_gather | solution.py:36
Sparse Core Ops, SparseCore 0:
  230.0 166.6 reduce-scatter.1
  399.0 164.0 all-gather.2
